TPU v7x, 32 devices: a whole 2x2x4 slice. The times are simulated.
32 devices in a mesh: seq: 8 (over z, y), head: 4 (over x, core).
Axes of the slice: x: 2, y: 2, z: 4, core: 2. Of those that a mesh axis runs over, the one named last changes fastest.
Arguments:
- byte_input: float32 [3072, 2048], P('seq', 'head'), may hold values from -6 to 6
- b_proj: float32 [3072, 128], P('seq'), may hold values from -1.25 to 1.25
- c_proj: float32 [3072, 128], P('seq'), may hold values from -1.25 to 1.25
- step_decay: float32 [32, 3072], P('head', 'seq'), may hold values from 0 to 1
- skip_gain: float32 [32], P('head'), may hold values from 0.5 to 1.5
- out_weight: bfloat16 [2048, 1024], P('head'), may hold values from -0.125 to 0.125
- boundaries: int32 [8, 128], P('seq'), may hold values from 0 to 383, as said below
- counts: int32 [8], P('seq'), may hold values from 0 to 128, as said below
- norm_gain: float32 [1024], replicated, may hold values from 0.1 to 1.9
- qkv_weight: bfloat16 [3, 1024, 2048], P(None, None, 'head'), may hold values from -1 to 1
Outputs:
- attended: float32 [512, 2048], P('seq', 'head')
Inputs may be any that keep to these rules, and one draw needn't show every extreme that they name: `boundaries`: row s holds counts[s] strictly increasing offsets, then zeros. The counts sum to 512; for every shard s the sum of the counts of shards before s lies within 32 of s * 64; some shard has 128.
All inputs are finite; a program needn't handle non-finite values.
Results may differ from a plain program's by a relative error of at most 0.0075.
Values may be sent and summed in bfloat16 or wider, within the bound.
A program may use at most 128 MiB of HBM per device.

v0:
```python
import jax
import jax.numpy as jnp
from jax import lax
from jax.sharding import PartitionSpec as P

ATT_DIM = 64
ROWS_DEV = 64


def prefix(shard, axis, combine, identity):
    length, here = (lax.axis_size(axis), lax.axis_index(axis))
    everything = jax.tree.map(lambda part: lax.all_gather(part, axis), shard)
    start = jax.tree.map(
        lambda part, zero: jnp.broadcast_to(jnp.asarray(zero, part.dtype), part.shape),
        shard,
        identity,
    )

    def lap(k, before):
        reached = k < here
        new = combine(before, jax.tree.map(lambda part: part[k], everything))
        return jax.tree.map(lambda a, b: jnp.where(reached, a, b), new, before)

    return lax.fori_loop(0, length, lap, start)


def extended(cells, sides, width):
    for axis, dim in sides:
        count = lax.axis_size(axis)
        ends = count - 1
        head = lax.slice_in_dim(cells, 0, width, axis=dim)
        tail = lax.slice_in_dim(cells, cells.shape[dim] - width, cells.shape[dim], axis=dim)
        cells = jnp.concatenate(
            [
                lax.ppermute(tail, axis, [(i, (i + 1) % count) for i in range(ends)]),
                cells,
                lax.ppermute(head, axis, [((i + 1) % count, i) for i in range(ends)]),
            ],
            axis=dim,
        )
    return cells


def state_space(inputs, b_rows, c_rows, decay):
    log_decay = jnp.cumsum(-decay, axis=1)
    affinity = jnp.dot(c_rows, b_rows.T, precision=lax.Precision.HIGHEST)
    length = inputs.shape[0]
    causal = lax.broadcasted_iota(jnp.int32, (length, length), 0) >= lax.broadcasted_iota(
        jnp.int32, (length, length), 1
    )

    def one_head(pair):
        values, logs = pair
        weights = (
            jnp.where(causal, jnp.exp(jnp.where(causal, logs[:, None] - logs[None, :], 0.0)), 0.0)
            * affinity
        )
        return jnp.dot(weights, values, precision=lax.Precision.HIGHEST)

    inside = lax.map(one_head, (inputs.transpose(1, 0, 2), log_decay))
    tail = jnp.exp(log_decay[:, -1:] - log_decay)
    own_state = jnp.einsum("ht,thp,tn->hpn", tail, inputs, b_rows, precision=lax.Precision.HIGHEST)
    return (log_decay, inside, own_state)


def link(earlier, later):
    return (earlier[0] * later[0], later[0][:, None, None] * earlier[1] + later[1])


def body(
    byte_input,
    b_proj,
    c_proj,
    step_decay,
    skip_gain,
    out_weight,
    boundaries,
    counts,
    norm_gain,
    qkv_weight,
):
    heads_here = step_decay.shape[0]
    length = byte_input.shape[0]
    inputs = byte_input.reshape(length, heads_here, -1)
    log_decay, inside, own_state = state_space(inputs, b_proj, c_proj, step_decay)
    span_decay = jnp.exp(log_decay[:, -1])
    arriving = prefix(
        (span_decay, own_state), "seq", link, (jnp.ones_like(span_decay), jnp.zeros_like(own_state))
    )
    carried = jnp.exp(log_decay)[:, :, None] * jnp.einsum(
        "tn,hpn->htp", c_proj, arriving[1], precision=lax.Precision.HIGHEST
    )
    mixed_heads = inside + carried + skip_gain[:, None, None] * inputs.transpose(1, 0, 2)
    slots = boundaries.shape[1]
    picked = jnp.take(mixed_heads, boundaries[0], axis=1)
    selected = picked.transpose(1, 0, 2).reshape(slots, -1).astype(jnp.bfloat16)
    all_counts = lax.all_gather(counts, "seq", axis=0, tiled=True)
    starts = jnp.cumsum(all_counts) - all_counts
    myself = lax.axis_index("seq")
    shards = lax.axis_size("seq")
    slot = jnp.arange(slots, dtype=jnp.int32)

    def slot_index(source):
        inside_axis = (source >= 0) & (source < shards)
        safe = jnp.clip(source, 0, shards - 1)
        begin = jnp.take(starts, safe)
        number = jnp.take(all_counts, safe)
        return jnp.where(inside_axis & (slot < number), begin + slot, -1)

    global_index = jnp.concatenate(
        [slot_index(myself - 1), slot_index(myself), slot_index(myself + 1)]
    )
    first_row = myself * ROWS_DEV
    target = first_row + jnp.arange(ROWS_DEV, dtype=jnp.int32)
    picker = global_index[None, :] == target[:, None]
    nearby = extended(selected, (("seq", 0),), slots)
    owned = jnp.dot(picker.astype(jnp.bfloat16), nearby, preferred_element_type=jnp.float32).astype(
        jnp.bfloat16
    )
    partial_value = jnp.dot(owned, out_weight, preferred_element_type=jnp.float32)
    packed = lax.psum(partial_value, "head")
    normed = (
        packed * lax.rsqrt(jnp.mean(packed * packed, axis=-1, keepdims=True) + 1e-05) * norm_gain
    ).astype(jnp.bfloat16)
    query = jnp.dot(normed, qkv_weight[0], preferred_element_type=jnp.float32).astype(jnp.bfloat16)
    keyed = jnp.dot(normed, qkv_weight[1], preferred_element_type=jnp.float32).astype(jnp.bfloat16)
    valued = jnp.dot(normed, qkv_weight[2], preferred_element_type=jnp.float32).astype(jnp.bfloat16)
    att_here = query.shape[1] // ATT_DIM
    queries = query.reshape(ROWS_DEV, att_here, ATT_DIM)
    row_place = first_row + jnp.arange(ROWS_DEV, dtype=jnp.int32)
    scale = ATT_DIM ** (-0.5)
    running = jnp.full((att_here, ROWS_DEV), -1e30, jnp.float32)
    key_piece = lax.all_gather(keyed, "seq", axis=0, tiled=True)
    value_piece = lax.all_gather(valued, "seq", axis=0, tiled=True)
    count = key_piece.shape[0]
    key_heads = key_piece.reshape(count, att_here, ATT_DIM)
    value_heads = value_piece.reshape(count, att_here, ATT_DIM)
    scores = (
        jnp.einsum("qhd,khd->hqk", queries, key_heads, preferred_element_type=jnp.float32) * scale
    )
    allowed = jnp.arange(count, dtype=jnp.int32)[None, :] <= row_place[:, None]
    scores = jnp.where(allowed[None], scores, -1e30)
    highest = jnp.maximum(running, jnp.max(scores, axis=-1))
    exps = jnp.where(allowed[None], jnp.exp(scores - highest[:, :, None]), 0.0)
    totals = jnp.sum(exps, axis=-1)
    weights = exps.astype(jnp.bfloat16)
    accum = jnp.einsum("hqk,khd->hqd", weights, value_heads, preferred_element_type=jnp.float32)
    running, totals, accum = (highest, totals, accum)
    result = accum / totals[:, :, None]
    return result.transpose(1, 0, 2).reshape(ROWS_DEV, att_here * ATT_DIM)


def solution(mesh):
    return jax.shard_map(
        body,
        mesh=mesh,
        in_specs=(
            P("seq", "head"),
            P("seq", None),
            P("seq", None),
            P("head", "seq"),
            P("head"),
            P("head", None),
            P("seq", None),
            P("seq"),
            P(),
            P(None, None, "head"),
        ),
        out_specs=P("seq", "head"),
        check_vma=False,
    )
```

profile of v0, /device:TPU:0, one launch (start us, length us, event | category | flops | bytes accessed | tf_op | source)
XLA Modules:
  0.0 200.7 jit_solution(14051487358311121036)
XLA Ops:
  6.5 0.0 all-gather.4.cloned.1.call-start
  6.6 0.8 negate_bitcast_fusion
  7.4 0.8 reduce-window.20
  8.3 0.2 slice_reduce_fusion
  8.5 0.1 fusion.62
  8.5 0.2 slice_reduce_fusion.1
  8.7 0.1 exponential_bitcast_fusion
  8.8 1.4 copy.39
  10.2 2.4 %fusion.32 = f32[8,64,128]{2,1,0:T(8,128)} fusion(f32[384,8,64]{0,2,1:T(8,128)S(1)} %bitcast.92, f32[384,8]{0,1:T(8,128)S(1)} %exponential_bitcast_fusion, f32[384,128]{1,0:T(8,128)} %param.15), kind=kOutput, calls=%fused_computation.43 | convolution fusion | flops 302186496 | bytes 1257472 | tf_op jit(solution)/shard_map/ht,thp,tn->hpn/dot_general | solution.py:62
  12.7 0.0 all-reduce.4.cloned.1.call-start
  13.4 0.6 dynamic-slice.18
  14.0 0.7 dynamic-update-slice.6
  14.7 13.2 %all-reduce = s32[8]{0:T(128)S(1)} all-reduce(s32[8]{0:T(128)S(1)} %dynamic-update-slice.6), channel_id=1, replica_groups=mesh['seq'=8,'head'=4] {'seq'}, use_global_device_ids=true, to_apply=%add | all-reduce | flops 8 | bytes 64
  27.9 0.2 reduce-window.19
  28.1 0.7 fusion.63
  33.2 0.2 dynamic-update-slice.7
  33.4 19.1 %all-reduce.1 = f32[64]{0:T(128)S(1)} all-reduce(f32[64]{0:T(128)S(1)} %dynamic-update-slice.7), channel_id=2, replica_groups=mesh['seq'=8,'head'=4] {'seq'}, use_global_device_ids=true, to_apply=%add.1 | all-reduce | flops 64 | bytes 512
  52.5 0.1 reshape.325
  52.7 1.5 fusion.66
  54.1 15.9 %while.32 = (s32[]{:T(128)}, f32[8,384,64]{1,2,0:T(8,128)S(1)}, f32[8,384]{1,0:T(8,128)S(1)}, f32[384,384]{1,0:T(8,128)}, f32[8,384,64]{1,2,0:T(8,128)S(1)}, /*index=5*/s32[]{:T(128)}) while((s32[]{:T(128)}, f32[8,384,64]{1,2,0:T(8,128)S(1)}, f32[8,384]{1,0:T(8,128)S(1)}, f32[384,384]{1,0:T(8,128)}, ...), condition=%wide.region_4.5_spmd.clone.clone, body=%wide.region_3.4_spmd.clone.clone.sunk | while | flops 113983488 | bytes 794697 | solution.py:60
  54.2 2.0 fusion.82
  56.2 2.0 fusion.82
  58.2 2.0 fusion.82
  60.2 2.0 fusion.82
  62.1 2.0 fusion.82
  64.1 2.0 fusion.82
  66.1 2.0 fusion.82
  68.1 2.0 fusion.82
  70.1 0.0 all-gather.4.cloned.1.call-done
  70.1 8.7 %while.33 = (s32[]{:T(128)}, f32[8,64,128]{2,1,0:T(8,128)S(1)}, s32[]{:T(128)}, f32[8,8]{1,0:T(8,128)S(1)}, f32[8,8,64,128]{3,2,1,0:T(8,128)}, /*index=5*/s32[]{:T(128)}, s32[]{:T(128)}) while((s32[]{:T(128)}, f32[8,64,128]{2,1,0:T(8,128)S(1)}, s32[]{:T(128)}, f32[8,8]{1,0:T(8,128)S(1)}, f32[8,8,64,128]{3,2,1,0:T(8,128)}, ...), condition=%wide.region_6.7_spmd.clone, body=%wide.region_5.6_spmd.clone.sunk | while | flops 262148 | bytes 786633 | solution.py:24
  70.2 1.1 fusion.83
  71.3 1.1 fusion.83
  72.3 1.1 fusion.83
  73.4 1.1 fusion.83
  74.5 1.1 fusion.83
  75.6 1.1 fusion.83
  76.7 1.1 fusion.83
  77.8 1.1 fusion.83
  78.9 0.8 fusion.21
  79.7 0.5 copy.41
  80.3 0.7 gather_fusion
  81.0 0.2 copy.42
  81.2 2.3 %collective-permute-start = (bf16[128,512]{0,1:T(8,128)(2,1)S(1)}, bf16[128,512]{0,1:T(8,128)(2,1)S(1)}, u32[]{:S(2)}, u32[]{:S(2)}) collective-permute-start(bf16[128,512]{0,1:T(8,128)(2,1)S(1)} %bitcast.97), channel_id=1, source_target_pairs={{0,4},{4,8},{8,12},{12,16},{16,20},{20,24},{24,28},{1,5},{5,9},{9,... | collective-permute-start | bytes 393224 | tf_op jit(solution)/shard_map/ppermute | solution.py:35
  83.5 1.3 collective-permute-start.1
  84.9 1.2 collective-permute-done
  86.0 4.4 %collective-permute-done.1 = bf16[128,512]{0,1:T(8,128)(2,1)S(1)} collective-permute-done((bf16[128,512]{0,1:T(8,128)(2,1)S(1)}, bf16[128,512]{0,1:T(8,128)(2,1)S(1)}, u32[]{:S(2)}, u32[]{:S(2)}) %collective-permute-start.1) | collective-permute-done | bytes 131104 | tf_op jit(solution)/shard_map/ppermute | solution.py:37
  90.4 1.2 fusion.23
  91.6 0.1 iota_compare_fusion.1
  91.7 29.9 %all-reduce.4.cloned.1.call-done = f32[64,1024]{1,0:T(8,128)} async-done(((f32[64,1024]{1,0:T(8,128)}), f32[64,1024]{1,0:T(8,128)}) %all-reduce.4.cloned.1.call-update) | async-done | bytes 262160 | tf_op jit(solution)/shard_map/psum | solution.py:121
  121.6 1.1 multiply_reduce_fusion
  122.7 1.0 multiply_convert_fusion
  123.8 1.5 convolution_convert_fusion.1
  125.3 1.5 convolution_convert_fusion.2
  126.8 1.5 convolution_convert_fusion
  128.4 31.7 %all_gather.23 = bf16[512,512]{1,0:T(8,128)(2,1)S(1)} all-gather(bf16[64,512]{1,0:T(8,128)(2,1)S(1)} %convolution_convert_fusion.1), channel_id=1, replica_groups=mesh['seq'=8,'head'=4] {'seq'}, dimensions={0}, use_global_device_ids=true | all-gather | bytes 589824 | tf_op jit(solution)/shard_map/all_gather | solution.py:133
  160.0 0.2 copy.43
  160.3 0.1 reshape.157
  160.4 0.4 fusion.65
  160.8 31.2 %all_gather.24 = bf16[512,512]{1,0:T(8,128)(2,1)S(1)} all-gather(bf16[64,512]{1,0:T(8,128)(2,1)S(1)} %convolution_convert_fusion), channel_id=1, replica_groups=mesh['seq'=8,'head'=4] {'seq'}, dimensions={0}, use_global_device_ids=true | all-gather | bytes 589824 | tf_op jit(solution)/shard_map/all_gather | solution.py:134
  192.0 0.2 copy.45
  192.2 0.4 fusion.30
  192.5 0.4 fusion.22
  192.9 0.2 copy.46
  193.1 0.8 reshape.160
  (49 shorter events, 0.4 us)
Async XLA Ops:
  6.5 83.9 %copy-start = (bf16[512,1024]{1,0:T(8,128)(2,1)S(1)}, bf16[512,1024]{1,0:T(8,128)(2,1)}, u32[]{:S(2)}) copy-start(bf16[512,1024]{1,0:T(8,128)(2,1)} %param.19) | copy-start | bytes 3145732
  6.5 6.8 %copy-start.6 = (u32[32]{0:T(128)S(1)}, u32[32]{0:T(128)}, u32[]{:S(2)}) copy-start(u32[32]{0:T(128)} %constant.266) | copy-start | bytes 388
  6.5 46.1 %copy-start.1 = (f32[384,128]{1,0:T(8,128)S(1)}, f32[384,128]{1,0:T(8,128)}, u32[]{:S(2)}) copy-start(f32[384,128]{1,0:T(8,128)} %param.15) | copy-start | bytes 589828
  6.5 46.1 %copy-start.5 = (s32[1,128]{1,0:T(1,128)S(1)}, s32[1,128]{1,0:T(1,128)}, u32[]{:S(2)}) copy-start(s32[1,128]{1,0:T(1,128)} %param.20) | copy-start | bytes 1540
  6.5 46.1 %copy-start.2 = (f32[384,128]{1,0:T(8,128)S(1)}, f32[384,128]{1,0:T(8,128)}, u32[]{:S(2)}) copy-start(f32[384,128]{1,0:T(8,128)} %param.16) | copy-start | bytes 589828
  6.5 63.6 %all-gather.4.cloned.1.call-start = ((), (), s32[]{:S(2)}) async-start(), calls=%async_computation.1 | async-start | bytes 2359296 | tf_op jit(solution)/shard_map/all_gather | solution.py:12
  12.7 109.0 %all-reduce.4.cloned.1.call-start = ((), (), s32[]{:S(2)}) async-start(), calls=%async_computation | async-start | bytes 524288 | tf_op jit(solution)/shard_map/psum | solution.py:121
  70.1 8.8 %copy-start.4 = (f32[8]{0:T(128)S(1)}, f32[8]{0:T(128)}, u32[]{:S(2)}) copy-start(f32[8]{0:T(128)} %param.18) | copy-start | bytes 100
  78.9 43.8 %copy-start.3 = (f32[1024]{0:T(1024)S(1)}, f32[1024]{0:T(1024)}, u32[]{:S(2)}) copy-start(f32[1024]{0:T(1024)} %param.22) | copy-start | bytes 12292
  81.2 4.8 %collective-permute-start = (bf16[128,512]{0,1:T(8,128)(2,1)S(1)}, bf16[128,512]{0,1:T(8,128)(2,1)S(1)}, u32[]{:S(2)}, u32[]{:S(2)}) collective-permute-start(bf16[128,512]{0,1:T(8,128)(2,1)S(1)} %bitcast.97), channel_id=1, source_target_pairs={{0,4},{4,8},{8,12},{12,16},{16,20},{20,24},{24,28},{1,5},{5,9},{9,... | collective-permute-start | bytes 393224 | tf_op jit(solution)/shard_map/ppermute | solution.py:35
  83.5 6.9 %collective-permute-start.1 = (bf16[128,512]{0,1:T(8,128)(2,1)S(1)}, bf16[128,512]{0,1:T(8,128)(2,1)S(1)}, u32[]{:S(2)}, u32[]{:S(2)}) collective-permute-start(bf16[128,512]{0,1:T(8,128)(2,1)S(1)} %bitcast.98), channel_id=1, source_target_pairs={{4,0},{8,4},{12,8},{16,12},{20,16},{24,20},{28,24},{5,1},{9,5},{13... | collective-permute-start | bytes 393224 | tf_op jit(solution)/shard_map/ppermute | solution.py:37
Sparse Core Ops, SparseCore 0:
  12.8 51.8 all-gather.3
  91.8 29.8 all-reduce.3
where the time goes:
time: 202 us; the launch traced here: 201 us
  blocking collectives  95.2 us (47%)
  waiting for transfers between devices  35.5 us (18%)
  matrix products  26.9 us (13%)
  between operations  18.8 us (9%)
  other arithmetic  13.1 us (6%)
  local copies, waits for them, and re-layouts  7.22 us (4%)
  starting transfers between devices  3.71 us (2%)
    unnamed x2, blocking collectives  32.3 us
    all_gather x1, blocking collectives, body(): key_piece = lax.all_gather(keyed, 'seq', axis=0, tiled=True)  31.7 us
    all_gather x1, blocking collectives, body(): value_piece = lax.all_gather(valued, 'seq', axis=0, tiled=True)  31.2 us
    psum x1, waiting for transfers between devices, body(): packed = lax.psum(partial_value, 'head')  29.9 us
    dot_general x8, matrix products, one_head(): return jnp.dot(weights, values, precision=lax.Precision.HIGHEST)  15.7 us
    select_n x8, other arithmetic, lap(): return jax.tree.map(lambda a, b: jnp.where(reached, a, b), new, before)  8.42 us
    ppermute x1, waiting for transfers between devices, extended(): lax.ppermute(head, axis, [((i + 1) % count, i) for i in range(ends)])  4.36 us
  transfers between devices with their start and end apart: 4, of which 3 were waited for; matrix products, arithmetic and copies ran while one was open for 10% of the time, Pallas kernels for 0%

commit v1 on v0

--- a/solution.py
+++ b/solution.py
@@ -1,6 +1,10 @@
+import functools
+
 import jax
 import jax.numpy as jnp
 from jax import lax
+from jax.experimental import pallas as pl
+from jax.experimental.pallas import tpu as pltpu
 from jax.sharding import PartitionSpec as P
 
 ATT_DIM = 64
@@ -150,9 +154,405 @@
     return result.transpose(1, 0, 2).reshape(ROWS_DEV, att_here * ATT_DIM)
 
 
+F32 = jnp.float32
+BF16 = jnp.bfloat16
+STATE_WIRE = jnp.float32
+PART_WIRE = jnp.float32
+EXTRA = 8
+
+
+def exact_dot(a, b, dims=((1,), (0,))):
+    return lax.dot_general(
+        a, b, (dims, ((), ())), precision=lax.Precision.HIGHEST, preferred_element_type=F32
+    )
+
+
+def fast_dot(a, b, dims=((1,), (0,))):
+    return lax.dot_general(a, b, (dims, ((), ())), preferred_element_type=F32)
+
+
+def halves(a):
+    high = a.astype(BF16)
+    return high, (a - high.astype(F32)).astype(BF16)
+
+
+def iota(shape, dim):
+    return lax.broadcasted_iota(jnp.int32, shape, dim)
+
+
+def fused(
+    seqs,
+    groups,
+    counts_ref,
+    skip_ref,
+    x_ref,
+    b_ref,
+    c_ref,
+    decay_ref,
+    bound_ref,
+    gain_ref,
+    outw_hbm,
+    qkvw_hbm,
+    out_ref,
+    outw,
+    qkvw,
+    send_a,
+    recv_a,
+    send_b,
+    recv_b,
+    send_p,
+    recv_p,
+    recv_n,
+    send_q,
+    recv_q,
+    send_o,
+    recv_o,
+    weight_sem,
+    a_sem,
+    b_sem,
+    p_send,
+    p_recv,
+    n_sem,
+    q_sem,
+    o_sem,
+):
+    me = lax.axis_index("seq")
+    col = lax.axis_index("head")
+    length, width = x_ref.shape
+    heads = decay_ref.shape[0]
+    lanes = width // heads
+    state = b_ref.shape[1]
+    slots = bound_ref.shape[1]
+    rows = out_ref.shape[0]
+    piece = rows // groups
+    half = rows // 2
+
+    outw_copy = pltpu.make_async_copy(outw_hbm, outw, weight_sem.at[0])
+    qkvw_copy = pltpu.make_async_copy(qkvw_hbm, qkvw, weight_sem.at[1])
+    outw_copy.start()
+    qkvw_copy.start()
+
+    def shard_at(d):
+        return lax.rem(me + d + seqs, seqs)
+
+    def head_at(d):
+        return lax.rem(col + d, groups)
+
+    barrier = pltpu.get_barrier_semaphore()
+    peers = [(shard_at(d), col) for d in range(1, seqs)]
+    peers += [(me, head_at(d)) for d in range(1, groups)]
+    peers += [(shard_at(e), head_at(d)) for e in (-1, 1) for d in range(1, groups)]
+    for peer in peers:
+        pl.semaphore_signal(
+            barrier, inc=1, device_id=peer, device_id_type=pl.DeviceIdType.MESH
+        )
+
+    def remote(src, dst, sems, k, peer):
+        return pltpu.make_async_remote_copy(
+            src_ref=src,
+            dst_ref=dst,
+            send_sem=sems.at[0, k],
+            recv_sem=sems.at[1, k],
+            device_id=peer,
+            device_id_type=pl.DeviceIdType.MESH,
+        )
+
+    decay = decay_ref[...]
+    upper = (iota((length, length), 0) <= iota((length, length), 1)).astype(F32)
+    lower = (iota((length, length), 0) >= iota((length, length), 1)).astype(F32)
+    logs = -exact_dot(decay, upper)
+    logs_t = -exact_dot(lower, decay, ((1,), (1,)))
+    first = iota((heads, width), 0) * lanes
+    channel = iota((heads, width), 1)
+    spread = ((channel >= first) & (channel < first + lanes)).astype(F32)
+    tail_t = jnp.exp(logs_t[length - 1 : length, :] - logs_t)
+    scaled = x_ref[...] * exact_dot(tail_t, spread)
+    own = exact_dot(scaled, b_ref[...], ((0,), (0,)))
+    number = jnp.full((EXTRA, state), counts_ref[0], jnp.int32).astype(F32)
+    for h in range(heads):
+        send_a[h, :lanes, :] = own[h * lanes : (h + 1) * lanes, :].astype(send_a.dtype)
+        last = jnp.broadcast_to(logs[h : h + 1, length - 1 : length], (EXTRA, state))
+        send_a[h, lanes:, :] = jnp.where(iota((EXTRA, state), 0) == 0, last, number)
+    pl.semaphore_wait(barrier, len(peers))
+    for d in range(1, seqs):
+        to = shard_at(d)
+        remote(send_a.at[to], recv_a.at[me], a_sem, d - 1, (to, col)).start()
+    recv_a[me] = send_a[me]
+
+    marks = jnp.broadcast_to(bound_ref[...].astype(F32), (slots, slots)).T
+    marks = jnp.concatenate([marks] * (length // slots), axis=1)
+    place = iota((slots, length), 1).astype(F32)
+    hit = place == marks
+    seen = place <= marks
+    onehot = hit.astype(F32)
+    c_rows = exact_dot(onehot, c_ref[...])
+    logs_sel = exact_dot(onehot, logs_t)
+    affinity = exact_dot(c_rows, b_ref[...], ((1,), (1,)))
+    inside = []
+    first_lane = iota((slots, 2 * lanes), 1) < lanes
+    for pair in range(heads // 2):
+        x_high, x_low = halves(x_ref[:, pair * 2 * lanes : (pair + 1) * 2 * lanes])
+        x_both = jnp.concatenate([x_high, x_low], axis=1)
+        parts = []
+        for h in (2 * pair, 2 * pair + 1):
+            gap = logs_sel[:, h : h + 1] - logs[h : h + 1, :]
+            weights = jnp.where(seen, jnp.exp(jnp.where(seen, gap, 0.0)), 0.0) * affinity
+            weights = weights + jnp.where(hit, skip_ref[h], 0.0)
+            w_high, w_low = halves(weights)
+            wide = fast_dot(w_high, x_both)
+            parts.append(
+                wide[:, : 2 * lanes] + wide[:, 2 * lanes :] + fast_dot(w_low, x_high)
+            )
+        inside.append(jnp.where(first_lane, parts[0], parts[1]))
+    inside = jnp.concatenate(inside, axis=1)
+    enter_scale = exact_dot(jnp.exp(logs_sel), spread)
+
+    for d in range(1, seqs):
+        source = shard_at(-d)
+        copy = remote(send_a.at[shard_at(d)], recv_a.at[source], a_sem, d - 1, (source, col))
+        copy.wait_recv()
+    running = jnp.zeros((lanes, state), F32)
+    for s in range(seqs):
+        send_b[s] = running.astype(send_b.dtype)
+        if s < seqs - 1:
+            kept = jnp.exp(recv_a[s, lanes : lanes + 1, :])
+            running = kept * running + recv_a[s, :lanes, :]
+    for d in range(1, seqs):
+        to = shard_at(d)
+        remote(send_b.at[to], recv_b.at[me], b_sem, d - 1, (to, col)).start()
+    recv_b[me] = send_b[me]
+
+    start = jnp.zeros((1, state), F32)
+    for s in range(seqs):
+        start = start + jnp.where(s < me, recv_a[s, lanes + 1 : lanes + 2, :], 0.0)
+    offset = start - (me * rows - half).astype(F32)
+    slot = iota((slots, slots), 1).astype(F32)
+    mine = jnp.full((slots, slots), counts_ref[0], jnp.int32).astype(F32)
+    shift = (slot == iota((slots, slots), 0).astype(F32) - offset) & (slot < mine)
+    shift = shift.astype(BF16)
+
+    for d in range(1, seqs):
+        source = shard_at(-d)
+        remote(send_b.at[shard_at(d)], recv_b.at[source], b_sem, d - 1, (source, col)).wait_recv()
+    entering = recv_b[...].reshape(heads * lanes, state).astype(F32)
+    c_high, c_low = halves(c_rows)
+    e_high, e_low = halves(entering)
+    last_dims = ((1,), (1,))
+    carried = (
+        fast_dot(c_high, e_high, last_dims)
+        + fast_dot(c_high, e_low, last_dims)
+        + fast_dot(c_low, e_high, last_dims)
+    )
+    y = (inside + enter_scale * carried).astype(BF16)
+    window = fast_dot(shift, y).astype(BF16)
+    outw_copy.wait()
+    partial = fast_dot(window, outw[...])
+    pieces = slots // piece
+    for i in range(pieces):
+        send_p[i] = partial[i * piece : (i + 1) * piece, :].astype(send_p.dtype)
+    outer = (pieces - groups) // 2
+
+    def project(src, slot, k, peer):
+        return pltpu.make_async_remote_copy(
+            src_ref=send_p.at[src],
+            dst_ref=recv_p.at[slot],
+            send_sem=p_send.at[k],
+            recv_sem=p_recv.at[slot],
+            device_id=peer,
+            device_id_type=pl.DeviceIdType.MESH,
+        )
+
+    sent = []
+    for i in range(outer):
+        sent.append(project(i, groups + col, i, (shard_at(-1), groups - outer + i)))
+        sent.append(
+            project(outer + groups + i, groups + col, outer + i, (shard_at(1), i))
+        )
+    for d in range(1, groups):
+        to = head_at(d)
+        sent.append(project(outer + to, col, 2 * outer + d - 1, (me, to)))
+    for copy in sent:
+        copy.start()
+    recv_p[col] = send_p[outer + col]
+    for d in range(1, groups):
+        source = head_at(groups - d)
+        project(0, source, 0, (me, source)).wait_recv()
+    for k in range(groups):
+        project(0, groups + k, 0, (shard_at(1), k)).wait_recv()
+    mixed = recv_p[0].astype(F32)
+    for k in range(1, 2 * groups):
+        mixed = mixed + recv_p[k].astype(F32)
+    square = jnp.mean(mixed * mixed, axis=-1, keepdims=True)
+    normed = (mixed * lax.rsqrt(square + 1e-05) * gain_ref[...]).astype(BF16)
+    recv_n[col] = normed
+    sent_n = []
+    for d in range(1, groups):
+        to = head_at(d)
+        sent_n.append(remote(recv_n.at[col], recv_n.at[col], n_sem, d - 1, (me, to)))
+        sent_n[-1].start()
+    for d in range(1, groups):
+        source = head_at(groups - d)
+        remote(recv_n.at[col], recv_n.at[source], n_sem, d - 1, (me, source)).wait_recv()
+    normed = recv_n[...].reshape(rows, -1)
+    qkvw_copy.wait()
+    query, key, value = [
+        fast_dot(normed, qkvw[i]).astype(BF16).astype(F32) for i in range(3)
+    ]
+    pair_width = 2 * lanes
+    left = iota((rows, pair_width), 1) < lanes
+    left_half = left[:half]
+
+    def turned(a):
+        return pltpu.roll(a, lanes, 1)
+
+    for pair in range(heads // 2):
+        at = slice(pair * pair_width, (pair + 1) * pair_width)
+        q, k, v = query[:, at], key[:, at], value[:, at]
+        send_q[2 * pair, :rows, :] = jnp.where(left, q, turned(k)).astype(BF16)
+        send_q[2 * pair + 1, :rows, :] = jnp.where(left, turned(q), k).astype(BF16)
+        above, below = v[:half], v[half:]
+        send_q[2 * pair, rows:, :] = jnp.where(left_half, above, turned(below)).astype(BF16)
+        send_q[2 * pair + 1, rows:, :] = jnp.where(
+            left_half, turned(above), below
+        ).astype(BF16)
+    for d in range(1, seqs):
+        to = shard_at(d)
+        remote(send_q.at[to], recv_q.at[me], q_sem, d - 1, (to, col)).start()
+    recv_q[me] = send_q[me]
+    for d in range(1, seqs):
+        source = shard_at(-d)
+        remote(send_q.at[shard_at(d)], recv_q.at[source], q_sem, d - 1, (source, col)).wait_recv()
+    coarse = seqs * rows
+    both = recv_q[:, :rows, :].reshape(coarse, pair_width)
+    wide = both.astype(F32)
+    left_all = iota((coarse, pair_width), 1) < lanes
+    queries = jnp.where(left_all, wide, 0.0).astype(BF16)
+    keys = turned(wide).astype(BF16)
+    values = []
+    for s in range(seqs):
+        packed = recv_q[s, rows:, :].astype(F32)
+        values += [packed, turned(packed)]
+    values = jnp.concatenate(values, axis=0).astype(BF16)
+    scores = fast_dot(queries, keys, ((1,), (1,))) * (lanes ** (-0.5))
+    allowed = iota((coarse, coarse), 0) >= iota((coarse, coarse), 1)
+    scores = jnp.where(allowed, scores, -1e30)
+    highest = jnp.max(scores, axis=-1, keepdims=True)
+    exps = jnp.where(allowed, jnp.exp(scores - highest), 0.0)
+    total = jnp.sum(exps, axis=-1, keepdims=True)
+    result = fast_dot(exps.astype(BF16), values) / total
+    for s in range(seqs):
+        above = result[s * rows : s * rows + half]
+        below = result[s * rows + half : (s + 1) * rows]
+        send_o[s] = jnp.where(left_half, above, turned(below))
+    for d in range(1, seqs):
+        to = shard_at(d)
+        remote(send_o.at[to], recv_o.at[me], o_sem, d - 1, (to, col)).start()
+    recv_o[me] = send_o[me]
+    for d in range(1, seqs):
+        source = shard_at(-d)
+        remote(send_o.at[shard_at(d)], recv_o.at[source], o_sem, d - 1, (source, col)).wait_recv()
+    for pair in range(heads // 2):
+        at = slice(pair * pair_width, (pair + 1) * pair_width)
+        even, odd = recv_o[2 * pair], recv_o[2 * pair + 1]
+        out_ref[:half, at] = jnp.where(left_half, even, turned(odd))
+        out_ref[half:, at] = jnp.where(left_half, turned(even), odd)
+
+    for copy in sent + sent_n:
+        copy.wait_send()
+    for sems, send, recv in (
+        (a_sem, send_a, recv_a),
+        (b_sem, send_b, recv_b),
+        (q_sem, send_q, recv_q),
+        (o_sem, send_o, recv_o),
+    ):
+        for d in range(1, seqs):
+            to = shard_at(d)
+            remote(send.at[to], recv.at[me], sems, d - 1, (to, col)).wait_send()
+
+
+def fused_body(
+    byte_input,
+    b_proj,
+    c_proj,
+    step_decay,
+    skip_gain,
+    out_weight,
+    boundaries,
+    counts,
+    norm_gain,
+    qkv_weight,
+):
+    seqs, groups = lax.axis_size("seq"), lax.axis_size("head")
+    heads = step_decay.shape[0]
+    width = byte_input.shape[1]
+    lanes = width // heads
+    state = b_proj.shape[1]
+    rows = ROWS_DEV
+    piece = rows // groups
+    enc = out_weight.shape[1]
+    pieces = boundaries.shape[1] // piece
+    vmem = pl.BlockSpec(memory_space=pltpu.VMEM)
+    smem = pl.BlockSpec(memory_space=pltpu.SMEM)
+    hbm = pl.BlockSpec(memory_space=pl.ANY)
+    dma = pltpu.SemaphoreType.DMA
+    return pl.pallas_call(
+        functools.partial(fused, seqs, groups),
+        out_shape=jax.ShapeDtypeStruct((rows, width), F32),
+        in_specs=[smem, smem] + [vmem] * 6 + [hbm] * 2,
+        out_specs=vmem,
+        scratch_shapes=[
+            pltpu.VMEM(out_weight.shape, BF16),
+            pltpu.VMEM(qkv_weight.shape, BF16),
+            pltpu.VMEM((seqs, lanes + EXTRA, state), STATE_WIRE),
+            pltpu.VMEM((seqs, lanes + EXTRA, state), STATE_WIRE),
+            pltpu.VMEM((seqs, lanes, state), STATE_WIRE),
+            pltpu.VMEM((seqs, lanes, state), STATE_WIRE),
+            pltpu.VMEM((pieces, piece, enc), PART_WIRE),
+            pltpu.VMEM((2 * groups, piece, enc), PART_WIRE),
+            pltpu.VMEM((groups, piece, enc), BF16),
+            pltpu.VMEM((seqs, rows + rows // 2, 2 * lanes), BF16),
+            pltpu.VMEM((seqs, rows + rows // 2, 2 * lanes), BF16),
+            pltpu.VMEM((seqs, rows // 2, 2 * lanes), F32),
+            pltpu.VMEM((seqs, rows // 2, 2 * lanes), F32),
+            dma((2,)),
+            dma((2, seqs - 1)),
+            dma((2, seqs - 1)),
+            dma((2 * groups,)),
+            dma((2 * groups,)),
+            dma((2, groups - 1)),
+            dma((2, seqs - 1)),
+            dma((2, seqs - 1)),
+        ],
+        compiler_params=pltpu.CompilerParams(collective_id=0, has_side_effects=True),
+    )(
+        counts,
+        skip_gain,
+        byte_input,
+        b_proj,
+        c_proj,
+        step_decay,
+        boundaries,
+        norm_gain.reshape(1, -1),
+        out_weight,
+        qkv_weight,
+    )
+
+
+def chosen(*args):
+    byte_input, step_decay, slots = args[0], args[3], args[6].shape[1]
+    heads = step_decay.shape[0]
+    lanes = byte_input.shape[1] // heads
+    seqs, groups = lax.axis_size("seq"), lax.axis_size("head")
+    fits = seqs == heads and lanes == ATT_DIM and args[9].shape[2] == byte_input.shape[1]
+    fits = fits and 2 * lanes == slots and args[1].shape[1] == slots and slots == 2 * ROWS_DEV
+    fits = fits and groups % 2 == 0 and ROWS_DEV % (16 * groups) == 0
+    fits = fits and byte_input.shape[0] % slots == 0
+    return fused_body(*args) if fits else body(*args)
+
+
 def solution(mesh):
     return jax.shard_map(
-        body,
+        chosen,
         mesh=mesh,
         in_specs=(
             P("seq", "head"),

time: 202 us -> 48 us (0.24)
  blocking collectives: 95.2 us -> 0 us
  Pallas kernels: 0 us -> 44.9 us
  waiting for transfers between devices: 35.5 us -> 0 us
  matrix products: 26.9 us -> 0 us
  between operations: 18.8 us -> 0.66 us
  other arithmetic: 13.1 us -> 0 us
  local copies, waits for them, and re-layouts: 7.22 us -> 1.57 us
  starting transfers between devices: 3.71 us -> 0 us
    all_gather x2 -> x0, blocking collectives: 62.9 us -> none  [the longest x1 31.7 us: body(): key_piece = lax.all_gather(keyed, 'seq', axis=0, tiled=True)]
    pallas_call x0 -> x1, Pallas kernels: none -> 44.9 us  [fused_body(): pl.pallas_call(functools.partial(fused, seqs, groups), out_shape=jax.Shap...]
    unnamed x2 -> x0, blocking collectives: 32.3 us -> none
    psum x1 -> x0, waiting for transfers between devices: 29.9 us -> none  [body(): packed = lax.psum(partial_value, 'head')]
    dot_general x17 -> x0, matrix products: 26.9 us -> none  [the longest x8 15.7 us: one_head(): return jnp.dot(weights, values, precision=lax.Precision.HIGHEST)]
    select_n x12 -> x0, other arithmetic: 8.44 us -> none  [the longest x8 8.42 us: lap(): return jax.tree.map(lambda a, b: jnp.where(reached, a, b), new, before)]
    ppermute x2 -> x0, waiting for transfers between devices: 5.53 us -> none  [the longest x1 4.36 us: extended(): lax.ppermute(head, axis, [((i + 1) % count, i) for i in range(ends)])]
    ppermute x2 -> x0, starting transfers between devices: 3.63 us -> none  [the longest x1 2.34 us: extended(): lax.ppermute(tail, axis, [(i, (i + 1) % count) for i in range(ends)])]
  transfers between devices with their start and end apart: 4 -> 0, of which waited for: 3 -> 0; matrix products, arithmetic and copies ran while one was open for 10% -> 0% of each run, Pallas kernels for 0% -> 0%
where the time goes in v1:
time: 48 us; the launch traced here: 47.1 us
  Pallas kernels  44.9 us (94%)
  local copies, waits for them, and re-layouts  1.57 us (3%)
  between operations  0.66 us (1%)
    pallas_call x1, Pallas kernels, fused_body(): pl.pallas_call(functools.partial(fused, seqs, groups), out_shape=jax.Shap...  44.9 us
    unnamed x1, local copies, waits for them, and re-layouts  1.57 us

profile of v1, /device:TPU:0, one launch (start us, length us, event | category | flops | bytes accessed | tf_op | source)
XLA Modules:
  0.0 47.1 jit_solution(8005225558013253130)
XLA Ops:
  0.7 44.9 %shard_map.100 = f32[64,512]{1,0:T(8,128)} custom-call(s32[1]{0:T(128)S(6)} %copy.12.counts_ref, f32[8]{0:T(128)} %skip_ref.1, f32[384,512]{1,0:T(8,128)} %x_ref.1, f32[384,128]{1,0:T(8,128)} %b_ref.1, f32[384,128]{1,0:T(8,128)} %c_ref.1, f32[8,384]{1,0:T(8,128)} %decay_ref.1, s32[1,128]{1,0:T(1,128)} %bound_ref.1, f32[1,1024]{1,0:T(1,128)} %bitcast.1, ...), custom_call_target="tpu_custom_call" | custom-call | tf_op jit(solution)/shard_map/pallas_call | solution.py:498
  45.6 1.6 %copy.13 = f32[64,512]{1,0:T(8,128)} copy(f32[64,512]{1,0:T(8,128)} %shard_map.100) | data formatting | bytes 262144

commit v2 on v1

--- a/solution.py
+++ b/solution.py
@@ -156,9 +156,10 @@
 
 F32 = jnp.float32
 BF16 = jnp.bfloat16
-STATE_WIRE = jnp.float32
-PART_WIRE = jnp.float32
-EXTRA = 8
+STATE_WIRE = jnp.bfloat16
+PART_WIRE = jnp.bfloat16
+OUT_WIRE = jnp.bfloat16
+EXTRA = 16
 
 
 def exact_dot(a, b, dims=((1,), (0,))):
@@ -183,18 +184,26 @@
 def fused(
     seqs,
     groups,
-    counts_ref,
-    skip_ref,
+    decay_hbm,
+    x_hbm,
+    b_hbm,
+    counts_hbm,
+    bound_hbm,
+    c_hbm,
+    skip_hbm,
+    outw_hbm,
+    gain_hbm,
+    qkvw_hbm,
+    out_ref,
+    decay_ref,
     x_ref,
     b_ref,
+    counts_ref,
+    bound_ref,
     c_ref,
-    decay_ref,
-    bound_ref,
+    skip_ref,
+    outw,
     gain_ref,
-    outw_hbm,
-    qkvw_hbm,
-    out_ref,
-    outw,
     qkvw,
     send_a,
     recv_a,
@@ -227,11 +236,6 @@
     piece = rows // groups
     half = rows // 2
 
-    outw_copy = pltpu.make_async_copy(outw_hbm, outw, weight_sem.at[0])
-    qkvw_copy = pltpu.make_async_copy(qkvw_hbm, qkvw, weight_sem.at[1])
-    outw_copy.start()
-    qkvw_copy.start()
-
     def shard_at(d):
         return lax.rem(me + d + seqs, seqs)
 
@@ -257,6 +261,27 @@
             device_id_type=pl.DeviceIdType.MESH,
         )
 
+    loads = [
+        pltpu.make_async_copy(source, target, weight_sem.at[i])
+        for i, (source, target) in enumerate(
+            (
+                (decay_hbm, decay_ref),
+                (x_hbm, x_ref),
+                (b_hbm, b_ref),
+                (counts_hbm, counts_ref),
+                (bound_hbm, bound_ref),
+                (c_hbm, c_ref),
+                (skip_hbm, skip_ref),
+                (outw_hbm, outw),
+                (gain_hbm, gain_ref),
+                (qkvw_hbm, qkvw),
+            )
+        )
+    ]
+    for load in loads:
+        load.start()
+
+    loads[0].wait()
     decay = decay_ref[...]
     upper = (iota((length, length), 0) <= iota((length, length), 1)).astype(F32)
     lower = (iota((length, length), 0) >= iota((length, length), 1)).astype(F32)
@@ -266,19 +291,31 @@
     channel = iota((heads, width), 1)
     spread = ((channel >= first) & (channel < first + lanes)).astype(F32)
     tail_t = jnp.exp(logs_t[length - 1 : length, :] - logs_t)
+    loads[1].wait()
+    loads[2].wait()
+    loads[3].wait()
     scaled = x_ref[...] * exact_dot(tail_t, spread)
     own = exact_dot(scaled, b_ref[...], ((0,), (0,)))
-    number = jnp.full((EXTRA, state), counts_ref[0], jnp.int32).astype(F32)
+    number = jnp.broadcast_to(counts_ref[...].astype(F32), (EXTRA, state))
+    extra_row = iota((EXTRA, state), 0)
     for h in range(heads):
         send_a[h, :lanes, :] = own[h * lanes : (h + 1) * lanes, :].astype(send_a.dtype)
         last = jnp.broadcast_to(logs[h : h + 1, length - 1 : length], (EXTRA, state))
-        send_a[h, lanes:, :] = jnp.where(iota((EXTRA, state), 0) == 0, last, number)
+        last_high, rest = halves(last)
+        rest = last - last_high.astype(F32)
+        last_mid, last_low = halves(rest)
+        extra = jnp.where(extra_row == 1, last_mid.astype(F32), last_high.astype(F32))
+        extra = jnp.where(extra_row == 2, last_low.astype(F32), extra)
+        extra = jnp.where(extra_row == 3, number, extra)
+        send_a[h, lanes:, :] = extra.astype(send_a.dtype)
     pl.semaphore_wait(barrier, len(peers))
     for d in range(1, seqs):
         to = shard_at(d)
         remote(send_a.at[to], recv_a.at[me], a_sem, d - 1, (to, col)).start()
     recv_a[me] = send_a[me]
 
+    for load in loads[4:7]:
+        load.wait()
     marks = jnp.broadcast_to(bound_ref[...].astype(F32), (slots, slots)).T
     marks = jnp.concatenate([marks] * (length // slots), axis=1)
     place = iota((slots, length), 1).astype(F32)
@@ -297,7 +334,7 @@
         for h in (2 * pair, 2 * pair + 1):
             gap = logs_sel[:, h : h + 1] - logs[h : h + 1, :]
             weights = jnp.where(seen, jnp.exp(jnp.where(seen, gap, 0.0)), 0.0) * affinity
-            weights = weights + jnp.where(hit, skip_ref[h], 0.0)
+            weights = weights + jnp.where(hit, skip_ref[:, h : h + 1], 0.0)
             w_high, w_low = halves(weights)
             wide = fast_dot(w_high, x_both)
             parts.append(
@@ -315,8 +352,9 @@
     for s in range(seqs):
         send_b[s] = running.astype(send_b.dtype)
         if s < seqs - 1:
-            kept = jnp.exp(recv_a[s, lanes : lanes + 1, :])
-            running = kept * running + recv_a[s, :lanes, :]
+            tags = recv_a[s, lanes:, :].astype(F32)
+            kept = jnp.exp((tags[0:1] + tags[1:2]) + tags[2:3])
+            running = kept * running + recv_a[s, :lanes, :].astype(F32)
     for d in range(1, seqs):
         to = shard_at(d)
         remote(send_b.at[to], recv_b.at[me], b_sem, d - 1, (to, col)).start()
@@ -324,28 +362,23 @@
 
     start = jnp.zeros((1, state), F32)
     for s in range(seqs):
-        start = start + jnp.where(s < me, recv_a[s, lanes + 1 : lanes + 2, :], 0.0)
+        start = start + jnp.where(s < me, recv_a[s, lanes:, :].astype(F32)[3:4], 0.0)
     offset = start - (me * rows - half).astype(F32)
     slot = iota((slots, slots), 1).astype(F32)
-    mine = jnp.full((slots, slots), counts_ref[0], jnp.int32).astype(F32)
+    mine = jnp.broadcast_to(counts_ref[...].astype(F32), (slots, slots))
     shift = (slot == iota((slots, slots), 0).astype(F32) - offset) & (slot < mine)
     shift = shift.astype(BF16)
 
     for d in range(1, seqs):
         source = shard_at(-d)
         remote(send_b.at[shard_at(d)], recv_b.at[source], b_sem, d - 1, (source, col)).wait_recv()
-    entering = recv_b[...].reshape(heads * lanes, state).astype(F32)
+    entering = recv_b[...].reshape(heads * lanes, state)
     c_high, c_low = halves(c_rows)
-    e_high, e_low = halves(entering)
     last_dims = ((1,), (1,))
-    carried = (
-        fast_dot(c_high, e_high, last_dims)
-        + fast_dot(c_high, e_low, last_dims)
-        + fast_dot(c_low, e_high, last_dims)
-    )
+    carried = fast_dot(c_high, entering, last_dims) + fast_dot(c_low, entering, last_dims)
     y = (inside + enter_scale * carried).astype(BF16)
     window = fast_dot(shift, y).astype(BF16)
-    outw_copy.wait()
+    loads[7].wait()
     partial = fast_dot(window, outw[...])
     pieces = slots // piece
     for i in range(pieces):
@@ -379,6 +412,7 @@
         project(0, source, 0, (me, source)).wait_recv()
     for k in range(groups):
         project(0, groups + k, 0, (shard_at(1), k)).wait_recv()
+    loads[8].wait()
     mixed = recv_p[0].astype(F32)
     for k in range(1, 2 * groups):
         mixed = mixed + recv_p[k].astype(F32)
@@ -394,7 +428,7 @@
         source = head_at(groups - d)
         remote(recv_n.at[col], recv_n.at[source], n_sem, d - 1, (me, source)).wait_recv()
     normed = recv_n[...].reshape(rows, -1)
-    qkvw_copy.wait()
+    loads[9].wait()
     query, key, value = [
         fast_dot(normed, qkvw[i]).astype(BF16).astype(F32) for i in range(3)
     ]
@@ -443,7 +477,7 @@
     for s in range(seqs):
         above = result[s * rows : s * rows + half]
         below = result[s * rows + half : (s + 1) * rows]
-        send_o[s] = jnp.where(left_half, above, turned(below))
+        send_o[s] = jnp.where(left_half, above, turned(below)).astype(send_o.dtype)
     for d in range(1, seqs):
         to = shard_at(d)
         remote(send_o.at[to], recv_o.at[me], o_sem, d - 1, (to, col)).start()
@@ -453,9 +487,9 @@
         remote(send_o.at[shard_at(d)], recv_o.at[source], o_sem, d - 1, (source, col)).wait_recv()
     for pair in range(heads // 2):
         at = slice(pair * pair_width, (pair + 1) * pair_width)
-        even, odd = recv_o[2 * pair], recv_o[2 * pair + 1]
-        out_ref[:half, at] = jnp.where(left_half, even, turned(odd))
-        out_ref[half:, at] = jnp.where(left_half, turned(even), odd)
+        even, odd = recv_o[2 * pair].astype(F32), recv_o[2 * pair + 1].astype(F32)
+        out_ref[:half, at] = jnp.where(left_half, even, turned(odd)).astype(OUT_WIRE)
+        out_ref[half:, at] = jnp.where(left_half, turned(even), odd).astype(OUT_WIRE)
 
     for copy in sent + sent_n:
         copy.wait_send()
@@ -492,17 +526,27 @@
     enc = out_weight.shape[1]
     pieces = boundaries.shape[1] // piece
     vmem = pl.BlockSpec(memory_space=pltpu.VMEM)
-    smem = pl.BlockSpec(memory_space=pltpu.SMEM)
     hbm = pl.BlockSpec(memory_space=pl.ANY)
     dma = pltpu.SemaphoreType.DMA
-    return pl.pallas_call(
+    operands = (
+        step_decay,
+        byte_input,
+        b_proj,
+        counts.reshape(1, 1),
+        boundaries,
+        c_proj,
+        skip_gain.reshape(1, -1),
+        out_weight,
+        norm_gain.reshape(1, -1),
+        qkv_weight,
+    )
+    result = pl.pallas_call(
         functools.partial(fused, seqs, groups),
-        out_shape=jax.ShapeDtypeStruct((rows, width), F32),
-        in_specs=[smem, smem] + [vmem] * 6 + [hbm] * 2,
+        out_shape=jax.ShapeDtypeStruct((rows, width), OUT_WIRE),
+        in_specs=[hbm] * len(operands),
         out_specs=vmem,
-        scratch_shapes=[
-            pltpu.VMEM(out_weight.shape, BF16),
-            pltpu.VMEM(qkv_weight.shape, BF16),
+        scratch_shapes=[pltpu.VMEM(array.shape, array.dtype) for array in operands]
+        + [
             pltpu.VMEM((seqs, lanes + EXTRA, state), STATE_WIRE),
             pltpu.VMEM((seqs, lanes + EXTRA, state), STATE_WIRE),
             pltpu.VMEM((seqs, lanes, state), STATE_WIRE),
@@ -512,9 +556,9 @@
             pltpu.VMEM((groups, piece, enc), BF16),
             pltpu.VMEM((seqs, rows + rows // 2, 2 * lanes), BF16),
             pltpu.VMEM((seqs, rows + rows // 2, 2 * lanes), BF16),
-            pltpu.VMEM((seqs, rows // 2, 2 * lanes), F32),
-            pltpu.VMEM((seqs, rows // 2, 2 * lanes), F32),
-            dma((2,)),
+            pltpu.VMEM((seqs, rows // 2, 2 * lanes), OUT_WIRE),
+            pltpu.VMEM((seqs, rows // 2, 2 * lanes), OUT_WIRE),
+            dma((len(operands),)),
             dma((2, seqs - 1)),
             dma((2, seqs - 1)),
             dma((2 * groups,)),
@@ -524,18 +568,8 @@
             dma((2, seqs - 1)),
         ],
         compiler_params=pltpu.CompilerParams(collective_id=0, has_side_effects=True),
-    )(
-        counts,
-        skip_gain,
-        byte_input,
-        b_proj,
-        c_proj,
-        step_decay,
-        boundaries,
-        norm_gain.reshape(1, -1),
-        out_weight,
-        qkv_weight,
-    )
+    )(*operands)
+    return result.astype(F32)
 
 
 def chosen(*args):

time: 48 us -> 41.1 us (0.86); the launches traced: 47.1 us -> 40.9 us
  Pallas kernels: 44.9 us -> 38.7 us
  local copies, waits for them, and re-layouts: 1.57 us -> 0 us
  other arithmetic: 0 us -> 1.5 us
    pallas_call x1, Pallas kernels: 44.9 us -> 38.7 us  [fused_body(): pl.pallas_call(functools.partial(fused, seqs, groups), out_shape=jax.Shap...]
    unnamed x1 -> x0, local copies, waits for them, and re-layouts: 1.57 us -> none
    convert_element_type x0 -> x1, other arithmetic: none -> 1.5 us  [fused_body(): return result.astype(F32)]
where the time goes in v2:
time: 41.1 us; the launch traced here: 40.9 us
  Pallas kernels  38.7 us (94%)
  other arithmetic  1.5 us (4%)
  between operations  0.66 us (2%)
    pallas_call x1, Pallas kernels, fused_body(): pl.pallas_call(functools.partial(fused, seqs, groups), out_shape=jax.Shap...  38.7 us
    convert_element_type x1, other arithmetic, fused_body(): return result.astype(F32)  1.5 us

profile of v2, /device:TPU:0, one launch (start us, length us, event | category | flops | bytes accessed | tf_op | source)
XLA Modules:
  0.0 40.9 jit_solution(10230734792267291735)
XLA Ops:
  0.7 38.7 %shard_map.100 = bf16[64,512]{1,0:T(8,128)(2,1)} custom-call(f32[8,384]{1,0:T(8,128)} %decay_hbm.1, f32[384,512]{1,0:T(8,128)} %x_hbm.1, f32[384,128]{1,0:T(8,128)} %b_hbm.1, s32[1,1]{1,0:T(1,128)} %bitcast.3.counts_hbm, s32[1,128]{1,0:T(1,128)} %bound_hbm.1, f32[384,128]{1,0:T(8,128)} %c_hbm.1, f32[1,8]{1,0:T(1,128)} %bitcast.5, ...), custom_call_target="tpu_custom_call" | custom-call | tf_op jit(solution)/shard_map/pallas_call | solution.py:543
  39.4 1.5 %convert_element_type.3 = f32[64,512]{1,0:T(8,128)} convert(bf16[64,512]{1,0:T(8,128)(2,1)} %shard_map.100) | non-fusion elementwise | flops 32768 | bytes 196608 | tf_op jit(solution)/shard_map/convert_element_type | solution.py:572

commit v3 on v2

--- a/solution.py
+++ b/solution.py
@@ -239,6 +239,21 @@
     def shard_at(d):
         return lax.rem(me + d + seqs, seqs)
 
+    layers = seqs // 2
+    mid = layers // 2
+    layer, side = me // 2, lax.rem(me, 2)
+    near_end = layer < mid
+    far_layers = [jnp.where(near_end, layers - 1 - k, k) for k in range(layers - mid)]
+    same = jnp.where(near_end, layer, layer - (layers - mid))
+    for k in range(1, mid):
+        turn = lax.rem(same + k, mid)
+        far_layers.append(jnp.where(near_end, turn, turn + (layers - mid)))
+    targets = []
+    for there in far_layers + [layer]:
+        targets.append(2 * there + 1 - side)
+        if there is not layer:
+            targets.append(2 * there + side)
+
     def head_at(d):
         return lax.rem(col + d, groups)
 
@@ -251,12 +266,12 @@
             barrier, inc=1, device_id=peer, device_id_type=pl.DeviceIdType.MESH
         )
 
-    def remote(src, dst, sems, k, peer):
+    def remote(src, dst, sems, k, source, peer):
         return pltpu.make_async_remote_copy(
             src_ref=src,
             dst_ref=dst,
             send_sem=sems.at[0, k],
-            recv_sem=sems.at[1, k],
+            recv_sem=sems.at[1, source],
             device_id=peer,
             device_id_type=pl.DeviceIdType.MESH,
         )
@@ -309,9 +324,8 @@
         extra = jnp.where(extra_row == 3, number, extra)
         send_a[h, lanes:, :] = extra.astype(send_a.dtype)
     pl.semaphore_wait(barrier, len(peers))
-    for d in range(1, seqs):
-        to = shard_at(d)
-        remote(send_a.at[to], recv_a.at[me], a_sem, d - 1, (to, col)).start()
+    for to in targets:
+        remote(send_a.at[to], recv_a.at[me], a_sem, to, me, (to, col)).start()
     recv_a[me] = send_a[me]
 
     for load in loads[4:7]:
@@ -346,7 +360,7 @@
 
     for d in range(1, seqs):
         source = shard_at(-d)
-        copy = remote(send_a.at[shard_at(d)], recv_a.at[source], a_sem, d - 1, (source, col))
+        copy = remote(send_a.at[shard_at(d)], recv_a.at[source], a_sem, source, source, (source, col))
         copy.wait_recv()
     running = jnp.zeros((lanes, state), F32)
     for s in range(seqs):
@@ -355,9 +369,8 @@
             tags = recv_a[s, lanes:, :].astype(F32)
             kept = jnp.exp((tags[0:1] + tags[1:2]) + tags[2:3])
             running = kept * running + recv_a[s, :lanes, :].astype(F32)
-    for d in range(1, seqs):
-        to = shard_at(d)
-        remote(send_b.at[to], recv_b.at[me], b_sem, d - 1, (to, col)).start()
+    for to in targets:
+        remote(send_b.at[to], recv_b.at[me], b_sem, to, me, (to, col)).start()
     recv_b[me] = send_b[me]
 
     start = jnp.zeros((1, state), F32)
@@ -371,7 +384,7 @@
 
     for d in range(1, seqs):
         source = shard_at(-d)
-        remote(send_b.at[shard_at(d)], recv_b.at[source], b_sem, d - 1, (source, col)).wait_recv()
+        remote(send_b.at[shard_at(d)], recv_b.at[source], b_sem, source, source, (source, col)).wait_recv()
     entering = recv_b[...].reshape(heads * lanes, state)
     c_high, c_low = halves(c_rows)
     last_dims = ((1,), (1,))
@@ -395,23 +408,44 @@
             device_id_type=pl.DeviceIdType.MESH,
         )
 
+    below_sent = [project(i, groups + col, i, (shard_at(-1), groups - outer + i)) for i in range(outer)]
+    above_sent = [
+        project(outer + groups + i, groups + col, outer + i, (shard_at(1), i))
+        for i in range(outer)
+    ]
     sent = []
-    for i in range(outer):
-        sent.append(project(i, groups + col, i, (shard_at(-1), groups - outer + i)))
-        sent.append(
-            project(outer + groups + i, groups + col, outer + i, (shard_at(1), i))
-        )
     for d in range(1, groups):
         to = head_at(d)
         sent.append(project(outer + to, col, 2 * outer + d - 1, (me, to)))
+    has_below, has_above = me > 0, me < seqs - 1
+
+    @pl.when(has_below)
+    def _():
+        for copy in below_sent:
+            copy.start()
+
+    @pl.when(has_above)
+    def _():
+        for copy in above_sent:
+            copy.start()
+
     for copy in sent:
         copy.start()
     recv_p[col] = send_p[outer + col]
+    expects = (has_below & (col < outer)) | (has_above & (col >= outer))
+
+    @pl.when(expects)
+    def _():
+        for k in range(groups):
+            project(0, groups + k, 0, (shard_at(1), k)).wait_recv()
+
+    @pl.when(jnp.logical_not(expects))
+    def _():
+        recv_p[groups:] = jnp.zeros((groups, piece, recv_p.shape[2]), recv_p.dtype)
+
     for d in range(1, groups):
         source = head_at(groups - d)
         project(0, source, 0, (me, source)).wait_recv()
-    for k in range(groups):
-        project(0, groups + k, 0, (shard_at(1), k)).wait_recv()
     loads[8].wait()
     mixed = recv_p[0].astype(F32)
     for k in range(1, 2 * groups):
@@ -422,11 +456,11 @@
     sent_n = []
     for d in range(1, groups):
         to = head_at(d)
-        sent_n.append(remote(recv_n.at[col], recv_n.at[col], n_sem, d - 1, (me, to)))
+        sent_n.append(remote(recv_n.at[col], recv_n.at[col], n_sem, to, col, (me, to)))
         sent_n[-1].start()
     for d in range(1, groups):
         source = head_at(groups - d)
-        remote(recv_n.at[col], recv_n.at[source], n_sem, d - 1, (me, source)).wait_recv()
+        remote(recv_n.at[col], recv_n.at[source], n_sem, source, source, (me, source)).wait_recv()
     normed = recv_n[...].reshape(rows, -1)
     loads[9].wait()
     query, key, value = [
@@ -449,13 +483,12 @@
         send_q[2 * pair + 1, rows:, :] = jnp.where(
             left_half, turned(above), below
         ).astype(BF16)
-    for d in range(1, seqs):
-        to = shard_at(d)
-        remote(send_q.at[to], recv_q.at[me], q_sem, d - 1, (to, col)).start()
+    for to in targets:
+        remote(send_q.at[to], recv_q.at[me], q_sem, to, me, (to, col)).start()
     recv_q[me] = send_q[me]
     for d in range(1, seqs):
         source = shard_at(-d)
-        remote(send_q.at[shard_at(d)], recv_q.at[source], q_sem, d - 1, (source, col)).wait_recv()
+        remote(send_q.at[shard_at(d)], recv_q.at[source], q_sem, source, source, (source, col)).wait_recv()
     coarse = seqs * rows
     both = recv_q[:, :rows, :].reshape(coarse, pair_width)
     wide = both.astype(F32)
@@ -478,13 +511,12 @@
         above = result[s * rows : s * rows + half]
         below = result[s * rows + half : (s + 1) * rows]
         send_o[s] = jnp.where(left_half, above, turned(below)).astype(send_o.dtype)
-    for d in range(1, seqs):
-        to = shard_at(d)
-        remote(send_o.at[to], recv_o.at[me], o_sem, d - 1, (to, col)).start()
+    for to in targets:
+        remote(send_o.at[to], recv_o.at[me], o_sem, to, me, (to, col)).start()
     recv_o[me] = send_o[me]
     for d in range(1, seqs):
         source = shard_at(-d)
-        remote(send_o.at[shard_at(d)], recv_o.at[source], o_sem, d - 1, (source, col)).wait_recv()
+        remote(send_o.at[shard_at(d)], recv_o.at[source], o_sem, source, source, (source, col)).wait_recv()
     for pair in range(heads // 2):
         at = slice(pair * pair_width, (pair + 1) * pair_width)
         even, odd = recv_o[2 * pair].astype(F32), recv_o[2 * pair + 1].astype(F32)
@@ -493,6 +525,17 @@
 
     for copy in sent + sent_n:
         copy.wait_send()
+
+    @pl.when(has_below)
+    def _():
+        for copy in below_sent:
+            copy.wait_send()
+
+    @pl.when(has_above)
+    def _():
+        for copy in above_sent:
+            copy.wait_send()
+
     for sems, send, recv in (
         (a_sem, send_a, recv_a),
         (b_sem, send_b, recv_b),
@@ -501,7 +544,7 @@
     ):
         for d in range(1, seqs):
             to = shard_at(d)
-            remote(send.at[to], recv.at[me], sems, d - 1, (to, col)).wait_send()
+            remote(send.at[to], recv.at[me], sems, to, me, (to, col)).wait_send()
 
 
 def fused_body(
@@ -559,13 +602,13 @@
             pltpu.VMEM((seqs, rows // 2, 2 * lanes), OUT_WIRE),
             pltpu.VMEM((seqs, rows // 2, 2 * lanes), OUT_WIRE),
             dma((len(operands),)),
-            dma((2, seqs - 1)),
-            dma((2, seqs - 1)),
+            dma((2, seqs)),
+            dma((2, seqs)),
             dma((2 * groups,)),
             dma((2 * groups,)),
-            dma((2, groups - 1)),
-            dma((2, seqs - 1)),
-            dma((2, seqs - 1)),
+            dma((2, groups)),
+            dma((2, seqs)),
+            dma((2, seqs)),
         ],
         compiler_params=pltpu.CompilerParams(collective_id=0, has_side_effects=True),
     )(*operands)
@@ -579,7 +622,7 @@
     seqs, groups = lax.axis_size("seq"), lax.axis_size("head")
     fits = seqs == heads and lanes == ATT_DIM and args[9].shape[2] == byte_input.shape[1]
     fits = fits and 2 * lanes == slots and args[1].shape[1] == slots and slots == 2 * ROWS_DEV
-    fits = fits and groups % 2 == 0 and ROWS_DEV % (16 * groups) == 0
+    fits = fits and seqs % 4 == 0 and groups % 2 == 0 and ROWS_DEV % (16 * groups) == 0
     fits = fits and byte_input.shape[0] % slots == 0
     return fused_body(*args) if fits else body(*args)
 

time: 41.1 us -> 40.2 us (0.978)
  Pallas kernels: 38.7 us -> 37.8 us
    pallas_call x1, Pallas kernels: 38.7 us -> 37.8 us  [fused_body(): pl.pallas_call(functools.partial(fused, seqs, groups), out_shape=jax.Shap...]
where the time goes in v3:
time: 40.2 us; the launch traced here: 40 us
  Pallas kernels  37.8 us (94%)
  other arithmetic  1.5 us (4%)
  between operations  0.66 us (2%)
    pallas_call x1, Pallas kernels, fused_body(): pl.pallas_call(functools.partial(fused, seqs, groups), out_shape=jax.Shap...  37.8 us
    convert_element_type x1, other arithmetic, fused_body(): return result.astype(F32)  1.5 us

profile of v3, /device:TPU:0, one launch (start us, length us, event | category | flops | bytes accessed | tf_op | source)
XLA Modules:
  0.0 40.0 jit_solution(1572526746156315396)
XLA Ops:
  0.7 37.8 %shard_map.100 = bf16[64,512]{1,0:T(8,128)(2,1)} custom-call(f32[8,384]{1,0:T(8,128)} %decay_hbm.1, f32[384,512]{1,0:T(8,128)} %x_hbm.1, f32[384,128]{1,0:T(8,128)} %b_hbm.1, s32[1,1]{1,0:T(1,128)} %bitcast.3.counts_hbm, s32[1,128]{1,0:T(1,128)} %bound_hbm.1, f32[384,128]{1,0:T(8,128)} %c_hbm.1, f32[1,8]{1,0:T(1,128)} %bitcast.5, ...), custom_call_target="tpu_custom_call" | custom-call | tf_op jit(solution)/shard_map/pallas_call | solution.py:586
  38.5 1.5 %convert_element_type.3 = f32[64,512]{1,0:T(8,128)} convert(bf16[64,512]{1,0:T(8,128)(2,1)} %shard_map.100) | non-fusion elementwise | flops 32768 | bytes 196608 | tf_op jit(solution)/shard_map/convert_element_type | solution.py:615

commit v4 on v3

--- a/solution.py
+++ b/solution.py
@@ -293,7 +293,7 @@
             )
         )
     ]
-    for load in loads:
+    for load in loads[:7]:
         load.start()
 
     loads[0].wait()
@@ -309,6 +309,8 @@
     loads[1].wait()
     loads[2].wait()
     loads[3].wait()
+    for load in loads[7:]:
+        load.start()
     scaled = x_ref[...] * exact_dot(tail_t, spread)
     own = exact_dot(scaled, b_ref[...], ((0,), (0,)))
     number = jnp.broadcast_to(counts_ref[...].astype(F32), (EXTRA, state))

time: 40.2 us -> 40.2 us (level)
  no operation moved by 1% of the time
where the time goes in v4:
time: 40.2 us; the launch traced here: 40 us
  Pallas kernels  37.8 us (94%)
  other arithmetic  1.5 us (4%)
  between operations  0.66 us (2%)
    pallas_call x1, Pallas kernels, fused_body(): pl.pallas_call(functools.partial(fused, seqs, groups), out_shape=jax.Shap...  37.8 us
    convert_element_type x1, other arithmetic, fused_body(): return result.astype(F32)  1.5 us

profile of v4, /device:TPU:0, one launch (start us, length us, event | category | flops | bytes accessed | tf_op | source)
XLA Modules:
  0.0 40.0 jit_solution(13713088214175613985)
XLA Ops:
  0.7 37.8 %shard_map.100 = bf16[64,512]{1,0:T(8,128)(2,1)} custom-call(f32[8,384]{1,0:T(8,128)} %decay_hbm.1, f32[384,512]{1,0:T(8,128)} %x_hbm.1, f32[384,128]{1,0:T(8,128)} %b_hbm.1, s32[1,1]{1,0:T(1,128)} %bitcast.3.counts_hbm, s32[1,128]{1,0:T(1,128)} %bound_hbm.1, f32[384,128]{1,0:T(8,128)} %c_hbm.1, f32[1,8]{1,0:T(1,128)} %bitcast.5, ...), custom_call_target="tpu_custom_call" | custom-call | tf_op jit(solution)/shard_map/pallas_call | solution.py:588
  38.5 1.5 %convert_element_type.3 = f32[64,512]{1,0:T(8,128)} convert(bf16[64,512]{1,0:T(8,128)(2,1)} %shard_map.100) | non-fusion elementwise | flops 32768 | bytes 196608 | tf_op jit(solution)/shard_map/convert_element_type | solution.py:617
